TPU v7x, 32 devices: a whole 2x2x4 slice. The times are simulated.
32 devices in a mesh: gx: 8 (over z, core), gy: 4 (over y, x).
Axes of the slice: x: 2, y: 2, z: 4, core: 2. Of those that a mesh axis runs over, the one named last changes fastest.
Arguments:
- density: float32 [256, 256, 256], P('gx', 'gy'), may hold values from 0.05 to 2
Outputs:
- potential: float32 [256, 256, 256], P('gx', 'gy')
- energy: float32 [], replicated
All inputs are finite; a program needn't handle non-finite values.
Results may differ from a plain program's by a relative error of at most 0.00005.
Values sent between devices are 32-bit elements.
A program may use at most 128 MiB of HBM per device.

v0:
```python
import math

import jax
import jax.numpy as jnp
from jax import lax
from jax.sharding import PartitionSpec as P

spacing = 1.0
highest = lax.Precision.HIGHEST
pbe_kappa = 0.804
pbe_mu = 0.2195149727645171
pbe_beta = 0.06672455060314922
pbe_gamma = 0.031090690869654894
pw_coef = 0.0310907
pw_alpha = 0.2137
pw_first = 7.5957
pw_second = 3.5876
pw_third = 1.6382
pw_fourth = 0.49294


def xc_energy(electrons, grad_sq):
    k_fermi = jnp.cbrt(3.0 * math.pi**2 * electrons)
    exch_unif = -0.75 * k_fermi / math.pi
    s_square = grad_sq / (4.0 * k_fermi**2 * electrons**2)
    enhance = 1.0 + pbe_kappa - pbe_kappa / (1.0 + pbe_mu * s_square / pbe_kappa)
    wigner = jnp.cbrt(3.0 / (4.0 * math.pi * electrons))
    root_rs = jnp.sqrt(wigner)
    series = (
        2.0
        * pw_coef
        * (
            pw_first * root_rs
            + pw_second * wigner
            + pw_third * wigner * root_rs
            + pw_fourth * wigner**2
        )
    )
    corr_unif = -2.0 * pw_coef * (1.0 + pw_alpha * wigner) * jnp.log(1.0 + 1.0 / series)
    screen_sq = 4.0 * k_fermi / math.pi
    t_square = grad_sq / (4.0 * screen_sq * electrons**2)
    factor = pbe_beta / pbe_gamma / jnp.expm1(-corr_unif / pbe_gamma)
    scaled = factor * t_square
    gradient_term = pbe_gamma * jnp.log(
        1.0 + pbe_beta / pbe_gamma * t_square * (1.0 + scaled) / (1.0 + scaled + scaled**2)
    )
    return electrons * (exch_unif * enhance + corr_unif + gradient_term)


def summed_energy(electrons, grad_sq):
    return jnp.sum(xc_energy(electrons, grad_sq))


def total_energy(energy_local, cells):
    return lax.psum(energy_local, ("gx", "gy")) / float(cells)


def wavenum(index, count):
    signed = jnp.where(index < count // 2, index, index - count)
    signed = jnp.where(index == count // 2, 0, signed)
    return signed.astype(jnp.float32) * (2.0 * math.pi / (count * spacing))


def dft_tables(count, order):
    columns = jnp.arange(count, dtype=jnp.int32)
    phase = (order[:, None] * columns[None, :] % count).astype(jnp.float32) * (
        2.0 * math.pi / count
    )
    return (jnp.cos(phase), jnp.sin(phase))


def deriv_matrix(count):
    positions = jnp.arange(count, dtype=jnp.int32)
    cosine, sine = dft_tables(count, positions)
    waves = wavenum(positions, count)
    first = jnp.dot(cosine.T * waves[None, :], sine, precision=highest)
    second = jnp.dot(sine.T * waves[None, :], cosine, precision=highest)
    return (first - second) / float(count)


def body(density):
    count_gx = lax.axis_size("gx")
    count_gy = lax.axis_size("gy")
    rows_x, rows_y, count_z = density.shape
    count_x = rows_x * count_gx
    count_y = rows_y * count_gy
    deriv_x = deriv_matrix(count_x)
    deriv_y = deriv_matrix(count_y)
    deriv_z = deriv_matrix(count_z)

    def line_x(piece):
        flat = piece.reshape(piece.shape[0], piece.shape[1] * piece.shape[2])
        result = jnp.dot(deriv_x, flat, precision=highest)
        return result.reshape(piece.shape)

    def line_y(piece):
        turned = jnp.swapaxes(piece, 0, 1)
        flat = turned.reshape(turned.shape[0], turned.shape[1] * turned.shape[2])
        result = jnp.dot(deriv_y, flat, precision=highest).reshape(turned.shape)
        return jnp.swapaxes(result, 0, 1)

    def along_x(field):
        lines = line_x(lax.all_to_all(field, "gx", split_axis=2, concat_axis=0, tiled=True))
        return lax.all_to_all(lines, "gx", split_axis=0, concat_axis=2, tiled=True)

    def along_y(field):
        lines = line_y(lax.all_to_all(field, "gy", split_axis=2, concat_axis=1, tiled=True))
        return lax.all_to_all(lines, "gy", split_axis=1, concat_axis=2, tiled=True)

    def along_z(field):
        flat = field.reshape(field.shape[0] * field.shape[1], field.shape[2])
        result = jnp.dot(flat, deriv_z.T, precision=highest)
        return result.reshape(field.shape)

    gradients = [along_x(density), along_y(density), along_z(density)]
    grad_sq = (
        gradients[0] * gradients[0] + gradients[1] * gradients[1] + gradients[2] * gradients[2]
    )
    energy_local, partials = jax.value_and_grad(summed_energy, argnums=(0, 1))(density, grad_sq)
    d_dens, d_grad = partials
    fluxes = [2.0 * d_grad * gradient for gradient in gradients]
    divergence = along_x(fluxes[0]) + along_y(fluxes[1]) + along_z(fluxes[2])
    potential = d_dens - divergence
    return (potential, total_energy(energy_local, count_x * count_y * count_z))


def solution(mesh):
    in_specs = (P("gx", "gy", None),)
    out_specs = (P("gx", "gy", None), P())
    return jax.shard_map(body, mesh=mesh, in_specs=in_specs, out_specs=out_specs, check_vma=False)
```

profile of v0, /device:TPU:9, one launch (start us, length us, event | category | flops | bytes accessed | tf_op | source)
XLA Modules:
  0.0 533.0 jit_solution(16059502869179916569)
XLA Ops:
  0.6 5.5 %copy.31 = f32[32,64,256]{1,0,2:T(8,128)} copy(f32[32,64,256]{2,1,0:T(8,128)} %param.1) | data formatting | bytes 4194304 | tf_op args[0]
  6.2 5.5 %reshape.56 = f32[4,1,131072]{2,1,0:T(1,128)} reshape(f32[256,32,64]{2,1,0:T(8,128)} %bitcast.101) | data formatting | bytes 4194304
  15.3 7.2 %reshape.60 = f32[8,1,65536]{2,1,0:T(1,128)} reshape(f32[256,32,64]{2,1,0:T(8,128)} %bitcast.102) | data formatting | bytes 4194304
  22.5 17.1 %all-to-all-done.2 = f32[4,1,131072]{2,1,0:T(1,128)S(1)} async-done(((f32[4,1,131072]{2,1,0:T(1,128)}), f32[4,1,131072]{2,1,0:T(1,128)S(1)}, u32[]{:S(2)}, u32[]{:S(2)}) %all-to-all-start.2) | async-done | bytes 2097184 | tf_op jit(solution)/shard_map/all_to_all | solution.py:107
  39.6 6.5 %all-to-all-start = ((f32[8,1,65536]{2,1,0:T(1,128)}), f32[8,1,65536]{2,1,0:T(1,128)}, u32[]{:S(2)}, u32[]{:S(2)}) async-start(f32[8,1,65536]{2,1,0:T(1,128)} %reshape.60), calls=%async_computation | async-start | bytes 4194304 | tf_op jit(solution)/shard_map/all_to_all | solution.py:103
  49.6 7.7 %reduce = f32[4,131072]{1,0:T(4,128)S(1)} reduce(f32[4,1,131072]{2,1,0:T(1,128)} %copy-done.2, f32[]{:T(128)} %broadcast.365), dimensions={1}, to_apply=%all_to_all.107.reduce_sub_computation | reduce | bytes 4194308 | tf_op jit(solution)/shard_map/all_to_all | solution.py:107
  57.3 3.9 reshape.57
  61.2 7.1 %copy.71 = f32[32,64,4,64]{1,2,3,0:T(4,128)} copy(f32[32,64,4,64]{1,0,3,2:T(8,128)} %bitcast.112) | data formatting | bytes 4194304 | tf_op jit(solution)/shard_map/all_to_all | solution.py:107
  68.2 4.2 all_to_all.110
  75.6 5.5 %copy.42 = f32[32,256,64]{2,0,1:T(8,128)} copy(f32[32,256,64]{1,2,0:T(8,128)} %fusion.18) | data formatting | bytes 4194304 | tf_op jit(solution)/shard_map/transpose | solution.py:100
  81.1 5.5 %reshape.58 = f32[4,1,131072]{2,1,0:T(1,128)} reshape(f32[256,32,64]{2,1,0:T(8,128)} %bitcast.106) | data formatting | bytes 4194304
  86.6 4.9 all-to-all-done
  91.5 4.7 all-to-all-start.3
  96.3 7.2 %reduce.2 = f32[8,65536]{1,0:T(8,128)S(1)} reduce(f32[8,1,65536]{2,1,0:T(1,128)} %all-to-all-done, f32[]{:T(128)} %broadcast.365), dimensions={1}, to_apply=%all_to_all.100.reduce_sub_computation | reduce | bytes 4194308 | tf_op jit(solution)/shard_map/all_to_all | solution.py:103
  107.1 7.0 %copy.33 = f32[8,32,64,32]{3,2,1,0:T(8,128)} copy(f32[8,32,64,32]{2,1,3,0:T(8,128)} %bitcast.104) | data formatting | bytes 4194304 | tf_op jit(solution)/shard_map/all_to_all | solution.py:103
  114.0 6.4 %reshape.49 = f32[256,2048]{1,0:T(8,128)S(1)} reshape(f32[8,32,64,32]{3,2,1,0:T(8,128)} %copy.33) | data formatting | bytes 4194304 | tf_op jit(solution)/shard_map/reshape | solution.py:92
  122.8 4.3 fusion.7
  127.1 4.4 copy.36
  131.6 7.2 %reshape.62 = f32[8,1,65536]{2,1,0:T(1,128)} reshape(f32[256,32,64]{2,1,0:T(8,128)} %bitcast.107) | data formatting | bytes 4194304
  138.8 8.0 %all-to-all-start.1 = ((f32[8,1,65536]{2,1,0:T(1,128)}), f32[8,1,65536]{2,1,0:T(1,128)}, u32[]{:S(2)}, u32[]{:S(2)}) async-start(f32[8,1,65536]{2,1,0:T(1,128)} %reshape.62), calls=%async_computation.1 | async-start | bytes 4194304 | tf_op jit(solution)/shard_map/all_to_all | solution.py:104
  153.1 9.0 %reduce.1 = f32[4,131072]{1,0:T(4,128)} reduce(f32[4,1,131072]{2,1,0:T(1,128)} %all-to-all-done.3, f32[]{:T(128)} %broadcast.365), dimensions={1}, to_apply=%all_to_all.111.reduce_sub_computation | reduce | bytes 4194308 | tf_op jit(solution)/shard_map/all_to_all | solution.py:108
  162.1 5.5 %reshape.59 = f32[256,32,64]{2,1,0:T(8,128)} reshape(f32[4,131072]{1,0:T(4,128)} %reduce.1) | data formatting | bytes 4194304
  167.6 6.9 %copy.70 = f32[32,4,64,64]{3,1,2,0:T(4,128)} copy(f32[32,4,64,64]{3,0,2,1:T(8,128)} %bitcast.114) | data formatting | bytes 4194304 | tf_op jit(solution)/shard_map/all_to_all | solution.py:108
  174.5 5.5 %all_to_all.114 = f32[32,64,256]{2,1,0:T(8,128)} reshape(f32[32,64,4,64]{3,2,1,0:T(4,128)} %bitcast.115) | data formatting | bytes 4194304 | tf_op jit(solution)/shard_map/all_to_all | solution.py:108
  179.9 12.4 %all-to-all-done.1 = f32[8,1,65536]{2,1,0:T(1,128)} async-done(((f32[8,1,65536]{2,1,0:T(1,128)}), f32[8,1,65536]{2,1,0:T(1,128)}, u32[]{:S(2)}, u32[]{:S(2)}) %all-to-all-start.1) | async-done | bytes 2097184 | tf_op jit(solution)/shard_map/all_to_all | solution.py:104
  192.3 8.5 %reduce.3 = f32[8,65536]{1,0:T(8,128)} reduce(f32[8,1,65536]{2,1,0:T(1,128)} %all-to-all-done.1, f32[]{:T(128)} %broadcast.365), dimensions={1}, to_apply=%all_to_all.103.reduce_sub_computation | reduce | bytes 4194308 | tf_op jit(solution)/shard_map/all_to_all | solution.py:104
  200.8 5.2 reshape.63
  206.0 4.8 copy.37
  210.8 3.8 copy.38
  214.6 11.6 %multiply_reduce_fusion = (f32[]{:T(128)}, f32[32,64,256]{2,1,0:T(8,128)S(1)}) fusion(f32[32,64,256]{2,1,0:T(8,128)S(1)} %copy-done, f32[32,64,256]{2,1,0:T(8,128)} %bitcast.128, f32[32,64,256]{2,1,0:T(8,128)} %all_to_all.114, f32[32,64,256]{2,1,0:T(8,128)} %copy.38), kind=kLoop, calls=%fused_computation.15 | loop fusion | flops 28311552 | bytes 10485764 | tf_op jit(solution)/shard_map/jvp()/reduce_sum | solution.py:51
  226.1 12.0 %fusion.60 = (f32[32,64,256]{2,1,0:T(8,128)}, f32[32,64,256]{2,1,0:T(8,128)}, f32[32,64,256]{2,1,0:T(8,128)}) fusion(f32[32,64,256]{2,1,0:T(8,128)S(1)} %copy-done.1, f32[32,64,256]{2,1,0:T(8,128)S(1)} %get-tuple-element.3, f32[32,64,256]{2,1,0:T(8,128)S(1)} %copy-done), kind=kLoop, calls=%fused_computation.85 | loop fusion | flops 37748736 | bytes 12582912 | tf_op jit(solution)/shard_map/mul | solution.py:121
  238.2 5.5 %copy.53 = f32[32,64,256]{1,0,2:T(8,128)} copy(f32[32,64,256]{2,1,0:T(8,128)} %get-tuple-element.4) | data formatting | bytes 4194304 | tf_op jit(solution)/shard_map/mul | solution.py:121
  243.7 5.5 %reshape.68 = f32[4,1,131072]{2,1,0:T(1,128)} reshape(f32[256,32,64]{2,1,0:T(8,128)} %bitcast.108) | data formatting | bytes 4194304
  249.2 4.5 all-to-all-start.6
  253.7 3.9 mul.496
  257.6 5.5 %copy.46 = f32[32,64,256]{1,0,2:T(8,128)} copy(f32[32,64,256]{2,1,0:T(8,128)} %mul.496) | data formatting | bytes 4194304 | tf_op jit(solution)/shard_map/mul | solution.py:121
  263.1 7.2 %reshape.64 = f32[8,1,65536]{2,1,0:T(1,128)} reshape(f32[256,32,64]{2,1,0:T(8,128)} %bitcast.109) | data formatting | bytes 4194304
  270.3 8.4 %all-to-all-done.6 = f32[4,1,131072]{2,1,0:T(1,128)} async-done(((f32[4,1,131072]{2,1,0:T(1,128)}), f32[4,1,131072]{2,1,0:T(1,128)}, u32[]{:S(2)}, u32[]{:S(2)}) %all-to-all-start.6) | async-done | bytes 2097184 | tf_op jit(solution)/shard_map/all_to_all | solution.py:107
  278.7 8.2 %all-to-all-start.4 = ((f32[8,1,65536]{2,1,0:T(1,128)}), f32[8,1,65536]{2,1,0:T(1,128)}, u32[]{:S(2)}, u32[]{:S(2)}) async-start(f32[8,1,65536]{2,1,0:T(1,128)} %reshape.64), calls=%async_computation.4 | async-start | bytes 4194304 | tf_op jit(solution)/shard_map/all_to_all | solution.py:103
  286.9 9.0 %reduce.6 = f32[4,131072]{1,0:T(4,128)} reduce(f32[4,1,131072]{2,1,0:T(1,128)} %all-to-all-done.6, f32[]{:T(128)} %broadcast.365), dimensions={1}, to_apply=%all_to_all.122.reduce_sub_computation | reduce | bytes 4194308 | tf_op jit(solution)/shard_map/all_to_all | solution.py:107
  296.0 5.5 %reshape.69 = f32[256,32,64]{2,1,0:T(8,128)} reshape(f32[4,131072]{1,0:T(4,128)} %reduce.6) | data formatting | bytes 4194304
  301.4 6.9 %copy.69 = f32[32,64,4,64]{1,2,3,0:T(4,128)} copy(f32[32,64,4,64]{1,0,3,2:T(8,128)} %bitcast.118) | data formatting | bytes 4194304 | tf_op jit(solution)/shard_map/all_to_all | solution.py:107
  308.3 5.7 %all_to_all.125 = f32[32,256,64]{1,2,0:T(8,128)} reshape(f32[32,4,64,64]{2,1,3,0:T(4,128)} %bitcast.119) | data formatting | bytes 4194304 | tf_op jit(solution)/shard_map/all_to_all | solution.py:107
  314.0 4.8 fusion.21
  318.7 5.5 %copy.55 = f32[32,256,64]{2,0,1:T(8,128)} copy(f32[32,256,64]{1,2,0:T(8,128)} %fusion.21) | data formatting | bytes 4194304 | tf_op jit(solution)/shard_map/transpose | solution.py:100
  324.2 5.5 %reshape.70 = f32[4,1,131072]{2,1,0:T(1,128)} reshape(f32[256,32,64]{2,1,0:T(8,128)} %bitcast.110) | data formatting | bytes 4194304
  332.4 4.4 all-to-all-start.7
  336.9 8.5 %reduce.4 = f32[8,65536]{1,0:T(8,128)} reduce(f32[8,1,65536]{2,1,0:T(1,128)} %all-to-all-done.4, f32[]{:T(128)} %broadcast.365), dimensions={1}, to_apply=%all_to_all.115.reduce_sub_computation | reduce | bytes 4194308 | tf_op jit(solution)/shard_map/all_to_all | solution.py:103
  345.4 5.2 reshape.65
  350.6 7.0 %copy.48 = f32[8,32,64,32]{3,2,1,0:T(8,128)} copy(f32[8,32,64,32]{2,1,3,0:T(8,128)} %bitcast.105) | data formatting | bytes 4194304 | tf_op jit(solution)/shard_map/all_to_all | solution.py:103
  357.6 7.5 %reshape.53 = f32[256,2048]{1,0:T(8,128)} reshape(f32[8,32,64,32]{3,2,1,0:T(8,128)} %copy.48) | data formatting | bytes 4194304 | tf_op jit(solution)/shard_map/reshape | solution.py:92
  368.1 5.6 %fusion.5 = f32[256,64,32]{0,1,2:T(8,128)} fusion(f32[64,32,256]{2,1,0:T(8,128)} %bitcast.127, f32[256,256]{1,0:T(8,128)S(1)} %fusion.26), kind=kOutput, calls=%fused_computation.11 | convolution fusion | flops 1610612736 | bytes 4456448 | tf_op jit(solution)/shard_map/dot_general | solution.py:93
  373.7 5.5 %copy.51 = f32[256,64,32]{1,2,0:T(8,128)} copy(f32[256,64,32]{0,1,2:T(8,128)} %fusion.5) | data formatting | bytes 4194304 | tf_op jit(solution)/shard_map/dot_general | solution.py:93
  379.3 7.2 %reshape.66 = f32[8,1,65536]{2,1,0:T(1,128)} reshape(f32[256,32,64]{2,1,0:T(8,128)} %bitcast.111) | data formatting | bytes 4194304
  386.5 7.9 %all-to-all-start.5 = ((f32[8,1,65536]{2,1,0:T(1,128)}), f32[8,1,65536]{2,1,0:T(1,128)}, u32[]{:S(2)}, u32[]{:S(2)}) async-start(f32[8,1,65536]{2,1,0:T(1,128)} %reshape.66), calls=%async_computation.5 | async-start | bytes 4194304 | tf_op jit(solution)/shard_map/all_to_all | solution.py:104
  394.4 66.8 %psum.7 = f32[]{:T(128)} all-reduce(f32[]{:T(128)} %get-tuple-element.2), channel_id=1, replica_groups=mesh['gx'=8,'gy'=4] {'gx','gy'}, use_global_device_ids=true, to_apply=%region_1.2 | all-reduce | flops 1 | bytes 8 | tf_op jit(solution)/shard_map/psum | solution.py:55
  461.8 9.0 %reduce.7 = f32[4,131072]{1,0:T(4,128)} reduce(f32[4,1,131072]{2,1,0:T(1,128)} %all-to-all-done.7, f32[]{:T(128)} %broadcast.365), dimensions={1}, to_apply=%all_to_all.126.reduce_sub_computation | reduce | bytes 4194308 | tf_op jit(solution)/shard_map/all_to_all | solution.py:108
  470.8 5.5 %reshape.71 = f32[256,32,64]{2,1,0:T(8,128)} reshape(f32[4,131072]{1,0:T(4,128)} %reduce.7) | data formatting | bytes 4194304
  476.3 6.9 %copy.68 = f32[32,4,64,64]{3,1,2,0:T(4,128)} copy(f32[32,4,64,64]{3,0,2,1:T(8,128)} %bitcast.120) | data formatting | bytes 4194304 | tf_op jit(solution)/shard_map/all_to_all | solution.py:108
  483.1 5.5 %all_to_all.129 = f32[32,64,256]{2,1,0:T(8,128)} reshape(f32[32,64,4,64]{3,2,1,0:T(4,128)} %bitcast.121) | data formatting | bytes 4194304 | tf_op jit(solution)/shard_map/all_to_all | solution.py:108
  488.6 8.5 %reduce.5 = f32[8,65536]{1,0:T(8,128)} reduce(f32[8,1,65536]{2,1,0:T(1,128)} %all-to-all-done.5, f32[]{:T(128)} %broadcast.365), dimensions={1}, to_apply=%all_to_all.118.reduce_sub_computation | reduce | bytes 4194308 | tf_op jit(solution)/shard_map/all_to_all | solution.py:104
  497.1 5.2 reshape.67
  502.3 4.8 copy.52
  510.9 20.8 %add_subtract_fusion = f32[32,64,256]{2,1,0:T(8,128)} fusion(f32[32,64,256]{2,1,0:T(8,128)} %copy.57, f32[32,64,256]{2,1,0:T(8,128)} %all_to_all.129, f32[32,64,256]{2,1,0:T(8,128)S(1)} %copy-done, f32[32,64,256]{2,1,0:T(8,128)} %copy-done.3, f32[32,64,256]{2,1,0:T(8,128)} %get-tuple-element.6, f32[32,64,256]{2,1,0:T(8,128)} %get-tuple-element.5, ...), kind=kOutput, calls=%fused_computation.16 | convolution fusion | flops 1688731648 | bytes 17039360 | tf_op jit(solution)/shard_map/dot_general | solution.py:112
  (24 shorter events, 32.0 us)
Async XLA Ops:
  11.6 28.0 %all-to-all-start.2 = ((f32[4,1,131072]{2,1,0:T(1,128)}), f32[4,1,131072]{2,1,0:T(1,128)S(1)}, u32[]{:S(2)}, u32[]{:S(2)}) async-start(f32[4,1,131072]{2,1,0:T(1,128)} %reshape.56), calls=%async_computation.2 | async-start | bytes 4194304 | tf_op jit(solution)/shard_map/all_to_all | solution.py:107
  39.6 6.5 %copy-start.2 = (f32[4,1,131072]{2,1,0:T(1,128)}, f32[4,1,131072]{2,1,0:T(1,128)S(1)}, u32[]{:S(2)}) copy-start(f32[4,1,131072]{2,1,0:T(1,128)S(1)} %all-to-all-done.2) | copy-start | bytes 6291460
  39.6 51.9 %all-to-all-start = ((f32[8,1,65536]{2,1,0:T(1,128)}), f32[8,1,65536]{2,1,0:T(1,128)}, u32[]{:S(2)}, u32[]{:S(2)}) async-start(f32[8,1,65536]{2,1,0:T(1,128)} %reshape.60), calls=%async_computation | async-start | bytes 4194304 | tf_op jit(solution)/shard_map/all_to_all | solution.py:103
  91.5 47.3 %all-to-all-start.3 = ((f32[4,1,131072]{2,1,0:T(1,128)}), f32[4,1,131072]{2,1,0:T(1,128)}, u32[]{:S(2)}, u32[]{:S(2)}) async-start(f32[4,1,131072]{2,1,0:T(1,128)} %reshape.58), calls=%async_computation.3 | async-start | bytes 4194304 | tf_op jit(solution)/shard_map/all_to_all | solution.py:108
  138.8 8.0 %copy-start = (f32[32,64,256]{2,1,0:T(8,128)S(1)}, f32[32,64,256]{2,1,0:T(8,128)}, u32[]{:S(2)}) copy-start(f32[32,64,256]{2,1,0:T(8,128)} %param.1) | copy-start | bytes 6291460
  138.8 53.5 %all-to-all-start.1 = ((f32[8,1,65536]{2,1,0:T(1,128)}), f32[8,1,65536]{2,1,0:T(1,128)}, u32[]{:S(2)}, u32[]{:S(2)}) async-start(f32[8,1,65536]{2,1,0:T(1,128)} %reshape.62), calls=%async_computation.1 | async-start | bytes 4194304 | tf_op jit(solution)/shard_map/all_to_all | solution.py:104
  214.6 11.6 %copy-start.1 = (f32[32,64,256]{2,1,0:T(8,128)S(1)}, f32[32,64,256]{2,1,0:T(8,128)}, u32[]{:S(2)}) copy-start(f32[32,64,256]{2,1,0:T(8,128)} %all_to_all.114) | copy-start | bytes 6291460
  226.1 12.0 %copy-start.3 = (f32[32,64,256]{2,1,0:T(8,128)}, f32[32,64,256]{2,1,0:T(8,128)S(1)}, u32[]{:S(2)}) copy-start(f32[32,64,256]{2,1,0:T(8,128)S(1)} %get-tuple-element.3) | copy-start | bytes 6291460
  249.2 29.5 %all-to-all-start.6 = ((f32[4,1,131072]{2,1,0:T(1,128)}), f32[4,1,131072]{2,1,0:T(1,128)}, u32[]{:S(2)}, u32[]{:S(2)}) async-start(f32[4,1,131072]{2,1,0:T(1,128)} %reshape.68), calls=%async_computation.6 | async-start | bytes 4194304 | tf_op jit(solution)/shard_map/all_to_all | solution.py:107
  278.7 53.7 %all-to-all-start.4 = ((f32[8,1,65536]{2,1,0:T(1,128)}), f32[8,1,65536]{2,1,0:T(1,128)}, u32[]{:S(2)}, u32[]{:S(2)}) async-start(f32[8,1,65536]{2,1,0:T(1,128)} %reshape.64), calls=%async_computation.4 | async-start | bytes 4194304 | tf_op jit(solution)/shard_map/all_to_all | solution.py:103
  332.4 54.1 %all-to-all-start.7 = ((f32[4,1,131072]{2,1,0:T(1,128)}), f32[4,1,131072]{2,1,0:T(1,128)}, u32[]{:S(2)}, u32[]{:S(2)}) async-start(f32[4,1,131072]{2,1,0:T(1,128)} %reshape.70), calls=%async_computation.7 | async-start | bytes 4194304 | tf_op jit(solution)/shard_map/all_to_all | solution.py:108
  386.5 102.1 %all-to-all-start.5 = ((f32[8,1,65536]{2,1,0:T(1,128)}), f32[8,1,65536]{2,1,0:T(1,128)}, u32[]{:S(2)}, u32[]{:S(2)}) async-start(f32[8,1,65536]{2,1,0:T(1,128)} %reshape.66), calls=%async_computation.5 | async-start | bytes 4194304 | tf_op jit(solution)/shard_map/all_to_all | solution.py:104
where the time goes:
time: 543 us; the launch traced here: 533 us
  local copies, waits for them, and re-layouts  230 us (42%)
  other arithmetic  95 us (17%)
  blocking collectives  66.8 us (12%)
  starting transfers between devices  47.8 us (9%)
  waiting for transfers between devices  45.5 us (8%)
  matrix products  44.7 us (8%)
    unnamed x25, local copies, waits for them, and re-layouts  96 us
    psum x1, blocking collectives, total_energy(): return lax.psum(energy_local, ('gx', 'gy')) / float(cells)  66.8 us
    all_to_all x2, waiting for transfers between devices, along_y(): lax.all_to_all(field, 'gy', split_axis=2, concat_axis=1, tiled=True)  25.5 us
    all_to_all x4, local copies, waits for them, and re-layouts, along_y(): return lax.all_to_all(lines, 'gy', split_axis=1, concat_axis=2, tiled=True)  24.6 us
    all_to_all x5, local copies, waits for them, and re-layouts, along_y(): lax.all_to_all(field, 'gy', split_axis=2, concat_axis=1, tiled=True)  24.3 us
    dot_general x2, matrix products, along_z(): result = jnp.dot(flat, deriv_z.T, precision=highest)  24 us
    all_to_all x2, other arithmetic, along_y(): return lax.all_to_all(lines, 'gy', split_axis=1, concat_axis=2, tiled=True)  18 us
    all_to_all x4, local copies, waits for them, and re-layouts, along_x(): return lax.all_to_all(lines, 'gx', split_axis=0, concat_axis=2, tiled=True)  17.2 us
  transfers between devices with their start and end apart: 8, of which 5 were waited for; matrix products, arithmetic and copies ran while one was open for 45% of the time, Pallas kernels for 0%

commit v1 on v0

v1 whole, which is shorter than its diff:
```python
import functools
import math

import jax
import jax.numpy as jnp
import numpy as np
from jax import lax
from jax.experimental import pallas as pl
from jax.experimental.pallas import tpu as pltpu
from jax.sharding import PartitionSpec as P

spacing = 1.0
highest = lax.Precision.HIGHEST
pbe_kappa = 0.804
pbe_mu = 0.2195149727645171
pbe_beta = 0.06672455060314922
pbe_gamma = 0.031090690869654894
pw_coef = 0.0310907
pw_alpha = 0.2137
pw_first = 7.5957
pw_second = 3.5876
pw_third = 1.6382
pw_fourth = 0.49294


def xc_energy(electrons, grad_sq):
    third = jnp.exp(jnp.log(electrons) * (1.0 / 3.0))
    k_fermi = (3.0 * math.pi**2) ** (1.0 / 3.0) * third
    exch_unif = -0.75 / math.pi * k_fermi
    inv_sq = grad_sq / (4.0 * k_fermi * electrons * electrons)
    s_square = inv_sq / k_fermi
    enhance = 1.0 + pbe_kappa - pbe_kappa / (1.0 + (pbe_mu / pbe_kappa) * s_square)
    wigner = (3.0 / (4.0 * math.pi)) ** (1.0 / 3.0) / third
    root_rs = jnp.sqrt(wigner)
    series = (
        2.0
        * pw_coef
        * root_rs
        * (pw_first + root_rs * (pw_second + root_rs * (pw_third + root_rs * pw_fourth)))
    )
    corr_unif = -2.0 * pw_coef * (1.0 + pw_alpha * wigner) * jnp.log(1.0 + 1.0 / series)
    t_square = inv_sq * (math.pi / 4.0)
    factor = (pbe_beta / pbe_gamma) / (jnp.exp(corr_unif * (-1.0 / pbe_gamma)) - 1.0)
    scaled = factor * t_square
    gradient_term = pbe_gamma * jnp.log(
        1.0 + (pbe_beta / pbe_gamma) * t_square * (1.0 + scaled) / (1.0 + scaled + scaled * scaled)
    )
    return electrons * (exch_unif * enhance + corr_unif + gradient_term)


def deriv_matrix(count):
    positions = np.arange(count)
    signed = np.where(positions < count // 2, positions, positions - count)
    signed = np.where(positions == count // 2, 0, signed)
    waves = signed * (2.0 * math.pi / (count * spacing))
    phase = (positions[:, None] * positions[None, :] % count) * (2.0 * math.pi / count)
    cosine, sine = np.cos(phase), np.sin(phase)
    first = (cosine.T * waves[None, :]) @ sine
    second = (sine.T * waves[None, :]) @ cosine
    return ((first - second) / count).astype(np.float32)


def far_first(count):
    return sorted(range(1, count), key=lambda k: abs(2 * k - count))


def kernel(
    num_gx, num_gy, zc,
    n_ref, dmx_ref, dmy_ref, dmz_ref,
    out_ref, energy_ref,
    n_t, lx1, rx1, gx_t, gx, ly1, ry1, gy, gz, fx_t, lx2, rx2, dx_t, ly2, ry2, dy,
    acc, part_y, tot_y, part_x,
    xs_sem, xr_sem, ys_sem, yr_sem, es_sem, er_sem,
):
    rows_x, rows_y, count_z = n_ref.shape
    block_y = rows_y // num_gx
    block_x = rows_x // num_gy
    count_x = rows_x * num_gx
    count_y = rows_y * num_gy
    chunks = count_z // zc
    me_x = lax.axis_index("gx")
    me_y = lax.axis_index("gy")

    def peer_x(k):
        return lax.rem(me_x + k, num_gx)

    def peer_y(k):
        return lax.rem(me_y + k, num_gy)

    def zs(c):
        return pl.ds(c * zc, zc)

    def x_block(i):
        return pl.ds(i * block_y, block_y)

    def x_rows(i):
        return pl.ds(pl.multiple_of(i * rows_x, rows_x), rows_x)

    def y_block(i):
        return pl.ds(i * block_x, block_x)

    def y_rows(i):
        return pl.ds(pl.multiple_of(i * rows_y, rows_y), rows_y)

    barrier = pltpu.get_barrier_semaphore()
    for k in range(1, num_gx):
        pl.semaphore_signal(
            barrier, inc=1, device_id={"gx": peer_x(k)}, device_id_type=pl.DeviceIdType.MESH
        )
    for k in range(1, num_gy):
        pl.semaphore_signal(
            barrier, inc=1, device_id={"gy": peer_y(k)}, device_id_type=pl.DeviceIdType.MESH
        )
    pl.semaphore_wait(barrier, num_gx + num_gy - 2)

    def send_x(phase, c, source, target, forward):
        copies = []
        for k in far_first(num_gx):
            to = peer_x(k)
            if forward:
                src, dst = source.at[x_block(to), :, zs(c)], target.at[:, x_rows(me_x), zs(c)]
            else:
                src, dst = source.at[:, x_rows(to), zs(c)], target.at[x_block(me_x), :, zs(c)]
            copy = pltpu.make_async_remote_copy(
                src_ref=src, dst_ref=dst,
                send_sem=xs_sem.at[phase, c, k], recv_sem=xr_sem.at[phase, c, k],
                device_id={"gx": to}, device_id_type=pl.DeviceIdType.MESH,
            )
            copy.start()
            copies.append(copy)
        if forward:
            target[:, x_rows(me_x), zs(c)] = source[x_block(me_x), :, zs(c)]
        else:
            target[x_block(me_x), :, zs(c)] = source[:, x_rows(me_x), zs(c)]
        return copies

    def send_y(phase, c, source, target, forward):
        copies = []
        for k in far_first(num_gy):
            to = peer_y(k)
            if forward:
                src, dst = source.at[y_block(to), :, zs(c)], target.at[:, y_rows(me_y), zs(c)]
            else:
                src, dst = source.at[:, y_rows(to), zs(c)], target.at[y_block(me_y), :, zs(c)]
            copy = pltpu.make_async_remote_copy(
                src_ref=src, dst_ref=dst,
                send_sem=ys_sem.at[phase, c, k], recv_sem=yr_sem.at[phase, c, k],
                device_id={"gy": to}, device_id_type=pl.DeviceIdType.MESH,
            )
            copy.start()
            copies.append(copy)
        if forward:
            target[:, y_rows(me_y), zs(c)] = source[y_block(me_y), :, zs(c)]
        else:
            target[y_block(me_y), :, zs(c)] = source[:, y_rows(me_y), zs(c)]
        return copies

    def arrived(copies):
        for copy in copies:
            copy.wait_recv()

    def lines(matrix, source, target, c):
        @pl.loop(0, source.shape[0])
        def _(i):
            target[i, :, zs(c)] = jnp.dot(
                matrix[...], source[i, :, zs(c)],
                precision=highest, preferred_element_type=jnp.float32,
            )

    step = min(8, rows_y)

    def turn_in(source, target, c):
        @pl.loop(0, rows_y // step)
        def _(j):
            y0 = pl.multiple_of(j * step, step)
            target[pl.ds(y0, step), :, zs(c)] = jnp.swapaxes(
                source[:, pl.ds(y0, step), zs(c)], 0, 1
            )

    def turn_out(source, target, c):
        @pl.loop(0, rows_y // step)
        def _(j):
            y0 = pl.multiple_of(j * step, step)
            target[:, pl.ds(y0, step), zs(c)] = jnp.swapaxes(
                source[pl.ds(y0, step), :, zs(c)], 0, 1
            )

    group = min(rows_x, max(1, 256 // rows_y))

    def along_z(source):
        def at(i):
            return pl.ds(i * group, group)

        def product(i):
            flat = source[at(i)].reshape(group * rows_y, count_z)
            result = jnp.dot(
                flat, dmz_ref[...], precision=highest, preferred_element_type=jnp.float32
            )
            return result.reshape(group, rows_y, count_z)

        return at, product

    sent = []
    every = range(chunks)
    fy1, fx1 = [], []
    for c in every:
        turn_in(n_ref, n_t, c)
        fx1.append(send_x(0, c, n_t, lx1, True))
        fy1.append(send_y(0, c, n_ref, ly1, True))
    at, product = along_z(n_ref)

    @pl.loop(0, rows_x // group)
    def _(i):
        gz[at(i)] = product(i)

    by1, bx1 = [], []
    for c in every:
        arrived(fy1[c])
        lines(dmy_ref, ly1, ry1, c)
        by1.append(send_y(1, c, ry1, gy, False))
    for c in every:
        arrived(fx1[c])
        lines(dmx_ref, lx1, rx1, c)
        bx1.append(send_x(1, c, rx1, gx_t, False))

    acc[...] = jnp.zeros_like(acc)
    part = min(rows_y, 32)
    fx2, fy2 = [], []
    for c in every:
        arrived(by1[c])
        arrived(bx1[c])
        turn_out(gx_t, gx, c)

        @pl.loop(0, rows_x)
        def _(i):
            @pl.loop(0, rows_y // part)
            def _(j):
                where = (i, pl.ds(pl.multiple_of(j * part, part), part), zs(c))
                dens, grad_x, grad_y, grad_z = n_ref[where], gx[where], gy[where], gz[where]
                grad_sq = grad_x * grad_x + grad_y * grad_y + grad_z * grad_z
                value, pull = jax.vjp(xc_energy, dens, grad_sq)
                d_dens, d_grad = pull(jnp.ones_like(value))
                twice = 2.0 * d_grad
                out_ref[where] = d_dens
                gx[where] = twice * grad_x
                gy[where] = twice * grad_y
                gz[where] = twice * grad_z
                acc[...] += value

        turn_in(gx, fx_t, c)
        fx2.append(send_x(2, c, fx_t, lx2, True))
        fy2.append(send_y(2, c, gy, ly2, True))

    energy = jnp.sum(acc[...].reshape(-1, 8, zc), axis=0)
    part_y[me_y] = energy
    energy_copies = []
    for k in range(1, num_gy):
        copy = pltpu.make_async_remote_copy(
            src_ref=part_y.at[me_y], dst_ref=part_y.at[me_y],
            send_sem=es_sem.at[0, k], recv_sem=er_sem.at[0, k],
            device_id={"gy": peer_y(k)}, device_id_type=pl.DeviceIdType.MESH,
        )
        copy.start()
        energy_copies.append(copy)

    at, product = along_z(gz)

    @pl.loop(0, rows_x // group)
    def _(i):
        out_ref[at(i)] = out_ref[at(i)] - product(i)

    arrived(energy_copies)
    sent.append(energy_copies)
    tot_y[...] = jnp.sum(part_y[...], axis=0)
    part_x[me_x] = tot_y[...]
    energy_copies = []
    for k in range(1, num_gx):
        copy = pltpu.make_async_remote_copy(
            src_ref=tot_y, dst_ref=part_x.at[me_x],
            send_sem=es_sem.at[1, k], recv_sem=er_sem.at[1, k],
            device_id={"gx": peer_x(k)}, device_id_type=pl.DeviceIdType.MESH,
        )
        copy.start()
        energy_copies.append(copy)

    bx2, by2 = [], []
    for c in every:
        arrived(fy2[c])
        lines(dmy_ref, ly2, ry2, c)
        by2.append(send_y(3, c, ry2, dy, False))
        arrived(fx2[c])
        lines(dmx_ref, lx2, rx2, c)
        bx2.append(send_x(3, c, rx2, dx_t, False))

    arrived(energy_copies)
    sent.append(energy_copies)
    energy_ref[...] = jnp.sum(part_x[...], axis=0)

    for c in every:
        arrived(by2[c])
        arrived(bx2[c])

        @pl.loop(0, rows_y // step)
        def _(j):
            y0 = pl.multiple_of(j * step, step)
            where = (slice(None), pl.ds(y0, step), zs(c))
            turned = jnp.swapaxes(dx_t[pl.ds(y0, step), :, zs(c)], 0, 1)
            out_ref[where] = out_ref[where] - (dy[where] + turned)

    for copies in sent + fx1 + fy1 + bx1 + by1 + fx2 + fy2 + bx2 + by2:
        for copy in copies:
            copy.wait_send()


def body(num_gx, num_gy, density):
    rows_x, rows_y, count_z = density.shape
    count_x = rows_x * num_gx
    count_y = rows_y * num_gy
    zc = 128 if count_z % 128 == 0 else count_z
    chunks = count_z // zc
    block_y = rows_y // num_gx
    block_x = rows_x // num_gy
    straight = (rows_x, rows_y, count_z)
    turned = (rows_y, rows_x, count_z)
    lines_x = (block_y, count_x, count_z)
    lines_y = (block_x, count_y, count_z)
    shapes = [
        turned, lines_x, lines_x, turned, straight,
        lines_y, lines_y, straight, straight,
        turned, lines_x, lines_x, turned,
        lines_y, lines_y, straight,
        (min(rows_y, 32), zc), (num_gy, 8, zc), (8, zc), (num_gx, 8, zc),
    ]
    vmem = pl.BlockSpec(memory_space=pltpu.VMEM)
    potential, partial = pl.pallas_call(
        functools.partial(kernel, num_gx, num_gy, zc),
        out_shape=(
            jax.ShapeDtypeStruct(straight, jnp.float32),
            jax.ShapeDtypeStruct((8, zc), jnp.float32),
        ),
        in_specs=[vmem] * 4,
        out_specs=(vmem, vmem),
        scratch_shapes=[pltpu.VMEM(shape, jnp.float32) for shape in shapes]
        + [
            pltpu.SemaphoreType.DMA((4, chunks, num_gx)),
            pltpu.SemaphoreType.DMA((4, chunks, num_gx)),
            pltpu.SemaphoreType.DMA((4, chunks, num_gy)),
            pltpu.SemaphoreType.DMA((4, chunks, num_gy)),
            pltpu.SemaphoreType.DMA((2, num_gx)),
            pltpu.SemaphoreType.DMA((2, num_gx)),
        ],
        compiler_params=pltpu.CompilerParams(
            collective_id=0, has_side_effects=True, vmem_limit_bytes=60 * 2**20
        ),
    )(
        density,
        jnp.asarray(deriv_matrix(count_x)),
        jnp.asarray(deriv_matrix(count_y)),
        jnp.asarray(deriv_matrix(count_z).T.copy()),
    )
    return (potential, jnp.sum(partial) / float(count_x * count_y * count_z))


def solution(mesh):
    in_specs = (P("gx", "gy", None),)
    out_specs = (P("gx", "gy", None), P())
    run = functools.partial(body, mesh.shape["gx"], mesh.shape["gy"])
    return jax.shard_map(run, mesh=mesh, in_specs=in_specs, out_specs=out_specs, check_vma=False)
```

time: 543 us -> 198 us (0.36); the launches traced: 533 us -> 198 us
  local copies, waits for them, and re-layouts: 230 us -> 3.13 us
  Pallas kernels: 0 us -> 191 us
  other arithmetic: 95 us -> 1.29 us
  blocking collectives: 66.8 us -> 0 us
  starting transfers between devices: 47.8 us -> 0 us
  waiting for transfers between devices: 45.5 us -> 0 us
  matrix products: 44.7 us -> 0 us
    pallas_call x0 -> x1, Pallas kernels: none -> 191 us  [body(): pl.pallas_call(functools.partial(kernel, num_gx, num_gy, zc), out_shape=(...]
    unnamed x25 -> x1, local copies, waits for them, and re-layouts: 96 us -> 3.13 us
    all_to_all x15 -> x0, local copies, waits for them, and re-layouts: 80 us -> none  [the longest x4 24.6 us: along_y(): return lax.all_to_all(lines, 'gy', split_axis=1, concat_axis=2, tiled=True)]
    all_to_all x8 -> x0, other arithmetic: 67.5 us -> none  [the longest x2 18 us: along_y(): return lax.all_to_all(lines, 'gy', split_axis=1, concat_axis=2, tiled=True)]
    psum x1 -> x0, blocking collectives: 66.8 us -> none  [total_energy(): return lax.psum(energy_local, ('gx', 'gy')) / float(cells)]
    all_to_all x8 -> x0, starting transfers between devices: 47.8 us -> none  [the longest x2 15.9 us: along_x(): return lax.all_to_all(lines, 'gx', split_axis=0, concat_axis=2, tiled=True)]
    all_to_all x8 -> x0, waiting for transfers between devices: 45.5 us -> none  [the longest x2 25.5 us: along_y(): lax.all_to_all(field, 'gy', split_axis=2, concat_axis=1, tiled=True)]
    dot_general x8 -> x0, matrix products: 44.7 us -> none  [the longest x2 24 us: along_z(): result = jnp.dot(flat, deriv_z.T, precision=highest)]
  transfers between devices with their start and end apart: 8 -> 0, of which waited for: 5 -> 0; matrix products, arithmetic and copies ran while one was open for 45% -> 0% of each run, Pallas kernels for 0% -> 0%
where the time goes in v1:
time: 198 us
  Pallas kernels  191 us (96%)
  local copies, waits for them, and re-layouts  3.13 us (2%)
  between operations  2.42 us (1%)
    pallas_call x1, Pallas kernels, body(): pl.pallas_call(functools.partial(kernel, num_gx, num_gy, zc), out_shape=(...  191 us

profile of v1, /device:TPU:9, one launch (start us, length us, event | category | flops | bytes accessed | tf_op | source)
XLA Modules:
  0.0 197.8 jit_solution(3688078011695896255)
XLA Ops:
  0.6 191.0 %shard_map.59 = (f32[32,64,256]{2,1,0:T(8,128)}, f32[8,128]{1,0:T(8,128)}) custom-call(f32[32,64,256]{2,1,0:T(8,128)} %n_ref.1, f32[256,256]{1,0:T(8,128)} %constant.9.clone.dmx_ref.dmy_ref, f32[256,256]{1,0:T(8,128)} %constant.9.clone.dmx_ref.dmy_ref, f32[256,256]{1,0:T(8,128)} %constant.10.clone.dmz_ref), custom_call_target="tpu_custom_call" | custom-call | tf_op jit(solution)/shard_map/pallas_call | solution.py:335
  191.6 1.3 reduce_sum.9
  193.6 3.1 %copy.7 = f32[32,64,256]{2,1,0:T(8,128)} copy(f32[32,64,256]{2,1,0:T(8,128)} %get-tuple-element.8) | data formatting | bytes 4194304

commit v2 on v1

--- a/solution.py
+++ b/solution.py
@@ -66,11 +66,12 @@
 
 def kernel(
     num_gx, num_gy, zc,
+    n_hbm, dmx_hbm, dmy_hbm, dmz_hbm,
+    out_ref, energy_ref,
     n_ref, dmx_ref, dmy_ref, dmz_ref,
-    out_ref, energy_ref,
     n_t, lx1, rx1, gx_t, gx, ly1, ry1, gy, gz, fx_t, lx2, rx2, dx_t, ly2, ry2, dy,
     acc, part_y, tot_y, part_x,
-    xs_sem, xr_sem, ys_sem, yr_sem, es_sem, er_sem,
+    xs_sem, xr_sem, ys_sem, yr_sem, es_sem, er_sem, in_sem,
 ):
     rows_x, rows_y, count_z = n_ref.shape
     block_y = rows_y // num_gx
@@ -102,6 +103,17 @@
     def y_rows(i):
         return pl.ds(pl.multiple_of(i * rows_y, rows_y), rows_y)
 
+    loads = [
+        pltpu.make_async_copy(n_hbm.at[:, :, zs(c)], n_ref.at[:, :, zs(c)], in_sem.at[c])
+        for c in range(chunks)
+    ]
+    pairs = ((dmz_hbm, dmz_ref), (dmy_hbm, dmy_ref), (dmx_hbm, dmx_ref))
+    tables = [
+        pltpu.make_async_copy(source, target, in_sem.at[chunks + place])
+        for place, (source, target) in enumerate(pairs)
+    ]
+    for copy in loads + tables:
+        copy.start()
     barrier = pltpu.get_barrier_semaphore()
     for k in range(1, num_gx):
         pl.semaphore_signal(
@@ -111,8 +123,6 @@
         pl.semaphore_signal(
             barrier, inc=1, device_id={"gy": peer_y(k)}, device_id_type=pl.DeviceIdType.MESH
         )
-    pl.semaphore_wait(barrier, num_gx + num_gy - 2)
-
     def send_x(phase, c, source, target, forward):
         copies = []
         for k in far_first(num_gx):
@@ -204,9 +214,14 @@
     every = range(chunks)
     fy1, fx1 = [], []
     for c in every:
+        loads[c].wait()
         turn_in(n_ref, n_t, c)
+        if c == 0:
+            pl.semaphore_wait(barrier, num_gx + num_gy - 2)
         fx1.append(send_x(0, c, n_t, lx1, True))
         fy1.append(send_y(0, c, n_ref, ly1, True))
+    for copy in tables:
+        copy.wait()
     at, product = along_z(n_ref)
 
     @pl.loop(0, rows_x // group)
@@ -294,7 +309,9 @@
 
     arrived(energy_copies)
     sent.append(energy_copies)
-    energy_ref[...] = jnp.sum(part_x[...], axis=0)
+    cells = float(count_x * count_y * count_z)
+    total = jnp.sum(part_x[...], axis=0)
+    energy_ref[...] = jnp.sum(total, axis=(0, 1), keepdims=True) * (1.0 / cells)
 
     for c in every:
         arrived(by2[c])
@@ -325,6 +342,7 @@
     lines_x = (block_y, count_x, count_z)
     lines_y = (block_x, count_y, count_z)
     shapes = [
+        straight, (count_x, count_x), (count_y, count_y), (count_z, count_z),
         turned, lines_x, lines_x, turned, straight,
         lines_y, lines_y, straight, straight,
         turned, lines_x, lines_x, turned,
@@ -335,10 +353,10 @@
     potential, partial = pl.pallas_call(
         functools.partial(kernel, num_gx, num_gy, zc),
         out_shape=(
-            jax.ShapeDtypeStruct(straight, jnp.float32),
-            jax.ShapeDtypeStruct((8, zc), jnp.float32),
+            pltpu.VMEM(straight, jnp.float32),
+            jax.ShapeDtypeStruct((1, 1), jnp.float32),
         ),
-        in_specs=[vmem] * 4,
+        in_specs=[pl.BlockSpec(memory_space=pltpu.HBM)] * 4,
         out_specs=(vmem, vmem),
         scratch_shapes=[pltpu.VMEM(shape, jnp.float32) for shape in shapes]
         + [
@@ -348,9 +366,10 @@
             pltpu.SemaphoreType.DMA((4, chunks, num_gy)),
             pltpu.SemaphoreType.DMA((2, num_gx)),
             pltpu.SemaphoreType.DMA((2, num_gx)),
+            pltpu.SemaphoreType.DMA((chunks + 3,)),
         ],
         compiler_params=pltpu.CompilerParams(
-            collective_id=0, has_side_effects=True, vmem_limit_bytes=60 * 2**20
+            collective_id=0, has_side_effects=True, vmem_limit_bytes=67043328 - 4 * density.size - 2**16
         ),
     )(
         density,
@@ -358,7 +377,7 @@
         jnp.asarray(deriv_matrix(count_y)),
         jnp.asarray(deriv_matrix(count_z).T.copy()),
     )
-    return (potential, jnp.sum(partial) / float(count_x * count_y * count_z))
+    return (potential, partial.reshape(()))
 
 
 def solution(mesh):

time: 198 us -> 192 us (0.970)
  Pallas kernels: 191 us -> 188 us
    pallas_call x1, Pallas kernels: 191 us -> 188 us  [body(): pl.pallas_call(functools.partial(kernel, num_gx, num_gy, zc), out_shape=(...]
where the time goes in v2:
time: 192 us
  Pallas kernels  188 us (98%)
  between operations  2.33 us (1%)
    pallas_call x1, Pallas kernels, body(): pl.pallas_call(functools.partial(kernel, num_gx, num_gy, zc), out_shape=(...  188 us

profile of v2, /device:TPU:9, one launch (start us, length us, event | category | flops | bytes accessed | tf_op | source)
XLA Modules:
  0.0 192.0 jit_solution(4591625897726223931)
XLA Ops:
  0.6 188.3 %shard_map.59 = (f32[32,64,256]{2,1,0:T(8,128)S(1)}, f32[1,1]{1,0:T(1,128)}) custom-call(f32[32,64,256]{2,1,0:T(8,128)} %n_hbm.1, f32[256,256]{1,0:T(8,128)} %constant.4.clone.dmx_hbm.dmy_hbm, f32[256,256]{1,0:T(8,128)} %constant.4.clone.dmx_hbm.dmy_hbm, f32[256,256]{1,0:T(8,128)} %constant.5.clone.dmz_hbm), custom_call_target="tpu_custom_call" | custom-call | tf_op jit(solution)/shard_map/pallas_call | solution.py:353
  189.0 1.3 copy.8

commit v3 on v2

--- a/solution.py
+++ b/solution.py
@@ -123,10 +123,12 @@
         pl.semaphore_signal(
             barrier, inc=1, device_id={"gy": peer_y(k)}, device_id_type=pl.DeviceIdType.MESH
         )
-    def send_x(phase, c, source, target, forward):
+    def send_x(phase, c, source, target, forward, prepare=None):
         copies = []
         for k in far_first(num_gx):
             to = peer_x(k)
+            if prepare is not None:
+                prepare(to)
             if forward:
                 src, dst = source.at[x_block(to), :, zs(c)], target.at[:, x_rows(me_x), zs(c)]
             else:
@@ -215,10 +217,21 @@
     fy1, fx1 = [], []
     for c in every:
         loads[c].wait()
-        turn_in(n_ref, n_t, c)
+        prepare = None
+        if block_y == step:
+
+            def prepare(to, c=c):
+                y0 = pl.multiple_of(to * step, step)
+                n_t[pl.ds(y0, step), :, zs(c)] = jnp.swapaxes(
+                    n_ref[:, pl.ds(y0, step), zs(c)], 0, 1
+                )
+
+            prepare(me_x)
+        else:
+            turn_in(n_ref, n_t, c)
         if c == 0:
             pl.semaphore_wait(barrier, num_gx + num_gy - 2)
-        fx1.append(send_x(0, c, n_t, lx1, True))
+        fx1.append(send_x(0, c, n_t, lx1, True, prepare))
         fy1.append(send_y(0, c, n_ref, ly1, True))
     for copy in tables:
         copy.wait()

time: 192 us -> 192 us (level)
  no operation moved by 1% of the time
where the time goes in v3:
time: 192 us
  Pallas kernels  188 us (98%)
  between operations  2.33 us (1%)
    pallas_call x1, Pallas kernels, body(): pl.pallas_call(functools.partial(kernel, num_gx, num_gy, zc), out_shape=(...  188 us

profile of v3, /device:TPU:9, one launch (start us, length us, event | category | flops | bytes accessed | tf_op | source)
XLA Modules:
  0.0 192.0 jit_solution(5082253669641099599)
XLA Ops:
  0.6 188.3 %shard_map.59 = (f32[32,64,256]{2,1,0:T(8,128)S(1)}, f32[1,1]{1,0:T(1,128)}) custom-call(f32[32,64,256]{2,1,0:T(8,128)} %n_hbm.1, f32[256,256]{1,0:T(8,128)} %constant.4.clone.dmx_hbm.dmy_hbm, f32[256,256]{1,0:T(8,128)} %constant.4.clone.dmx_hbm.dmy_hbm, f32[256,256]{1,0:T(8,128)} %constant.5.clone.dmz_hbm), custom_call_target="tpu_custom_call" | custom-call | tf_op jit(solution)/shard_map/pallas_call | solution.py:366
  189.0 1.3 copy.8
